TPU v7x, 32 devices: a whole 2x2x4 slice. The times are simulated.
32 devices in a mesh: section: 16 (over z, y, core), walk: 2 (over x).
Axes of the slice: x: 2, y: 2, z: 4, core: 2. Of those that a mesh axis runs over, the one named last changes fastest.
Arguments:
- fields: bfloat16 [16, 8, 800], P('section', None, 'walk'), may hold values from -4 to 4
- cholesky_vectors: bfloat16 [800, 200, 200], P('walk'), may hold values from -0.013 to 0.013
- trial_state: float32 [200, 100], replicated, may hold values from -1.6 to 1.6
- deviation: bfloat16 [16, 8, 200, 100], P('section', 'walk'), may hold values from -0.1796875 to 0.1796875
Outputs:
- density: float32 [8, 200, 200], P('walk')
All inputs are finite; a program needn't handle non-finite values.
Results may differ from a plain program's by a relative error of at most 0.0003.
Values sent between devices are 32-bit elements; how exact they have to be, the bound alone decides.
A program may use at most 128 MiB of HBM per device.

v0:
```python
import jax
import jax.numpy as jnp
from jax import lax
from jax.sharding import PartitionSpec as P

TAYLOR = 6
exact_mode = lax.Precision.HIGHEST


def entering(shard, axis, combine, identity):
    size, position = (lax.axis_size(axis), lax.axis_index(axis))
    everything = lax.all_gather(shard, axis)
    start = jnp.broadcast_to(jnp.asarray(identity, shard.dtype), shard.shape)

    def lap(k, before):
        at = size - 1 - k
        reached = at > position
        new = combine(before, everything[at])
        return jnp.where(reached, new, before)

    return lax.fori_loop(0, size, lap, start)


def series_matrix(field_matrix):
    orbitals = field_matrix.shape[-1]
    series_term = jnp.broadcast_to(jnp.eye(orbitals, dtype=jnp.float32), field_matrix.shape)
    summed = series_term
    for degree in range(1, TAYLOR + 1):
        series_term = (
            jnp.einsum("wij,wjk->wik", series_term, field_matrix, precision=exact_mode) / degree
        )
        summed = summed + series_term
    return summed


def solve_normal(factor, right_side):
    return jax.scipy.linalg.cho_solve((factor, True), right_side)


def green_block(left_state, walker):
    intersection = jnp.einsum("wie,wif->wef", left_state, walker, precision=exact_mode)
    normal_matrix = jnp.einsum("wef,weg->wfg", intersection, intersection, precision=exact_mode)
    right_side = jnp.einsum("wef,wie->wfi", intersection, left_state, precision=exact_mode)
    factor = jnp.linalg.cholesky(normal_matrix)
    solved = jax.vmap(solve_normal)(factor, right_side)
    return jnp.einsum("wie,wej->wij", walker, solved, precision=exact_mode)


def body(fields, cholesky_vectors, trial_state, deviation):
    steps_here, walker_count, chol_here = fields.shape
    orbitals = cholesky_vectors.shape[1]
    per_device = deviation.shape[1]
    field_rows = jnp.swapaxes(fields, 0, 1).reshape(walker_count * steps_here, chol_here)
    vector_table = cholesky_vectors.reshape(chol_here, orbitals * orbitals)
    field_matrices = lax.psum_scatter(
        jnp.dot(field_rows, vector_table, preferred_element_type=jnp.float32),
        "walk",
        scatter_dimension=0,
        tiled=True,
    )
    field_matrices = field_matrices.reshape(per_device, steps_here, orbitals, orbitals)
    walkers = trial_state + deviation.astype(jnp.float32)
    section_count = lax.axis_size("section")
    total_steps = steps_here * section_count
    series = [series_matrix(field_matrices[:, 0])]
    identity = jnp.broadcast_to(
        jnp.eye(orbitals, dtype=jnp.float32), (per_device, orbitals, orbitals)
    )
    block_map = identity
    for offset in reversed(range(steps_here)):
        block_map = jnp.einsum("wji,wjk->wik", series[offset], block_map, precision=exact_mode)

    def compose(earlier, later):
        return jnp.einsum("wij,wjk->wik", later, earlier, precision=exact_mode)

    prefix = entering(block_map, "section", compose, identity)
    incoming = jnp.einsum("wij,je->wie", prefix, trial_state, precision=exact_mode)
    left_state = incoming
    running = jnp.zeros((incoming.shape[0], orbitals, orbitals), jnp.float32)
    for offset in reversed(range(steps_here)):
        left_state = jnp.einsum("wji,wje->wie", series[offset], left_state, precision=exact_mode)
        running = running + green_block(left_state, walkers[offset])
    running, leaving = (running, left_state)
    summed = lax.psum(running, "section")
    return summed / total_steps


def solution(mesh):
    in_specs = (
        P("section", None, "walk"),
        P("walk", None, None),
        P(),
        P("section", "walk", None, None),
    )
    out_specs = P("walk", None, None)
    return jax.shard_map(body, mesh=mesh, in_specs=in_specs, out_specs=out_specs, check_vma=False)
```

profile of v0, /device:TPU:0, one launch (start us, length us, event | category | flops | bytes accessed | tf_op | source)
XLA Modules:
  0.0 450.3 jit_solution(12506095595911162128)
XLA Ops:
  6.5 57.5 %reshape.20 = bf16[400,40000]{1,0:T(8,128)(2,1)} reshape(bf16[400,200,200]{2,1,0:T(8,128)(2,1)} %param.7) | data formatting | bytes 64000000 | tf_op jit(solution)/shard_map/reshape | solution.py:54
  64.0 13.4 %fusion.22 = f32[8,40000]{1,0:T(8,128)} fusion(bf16[400,40000]{1,0:T(8,128)(2,1)} %reshape.20, bf16[1,8,400]{2,1,0:T(8,128)(2,1)S(1)} %copy-done), kind=kOutput, calls=%fused_computation.36 | convolution fusion | flops 256000000 | bytes 33286400 | tf_op jit(solution)/shard_map/dot_general | solution.py:56
  78.8 46.8 %all-reduce.6.cloned.1.call-done = f32[8,40000]{1,0:T(8,128)} async-done(((f32[8,40000]{1,0:T(8,128)}), f32[8,40000]{1,0:T(8,128)}) %all-reduce.6.cloned.1.call-update) | async-done | bytes 1280016
  133.5 2.6 fusion.8
  136.4 103.8 %all-gather.3.cloned.1.call-done = f32[64,200,200]{2,1,0:T(8,128)} async-done(((f32[4,200,200]{2,1,0:T(8,128)}), f32[64,200,200]{2,1,0:T(8,128)}) %all-gather.3.cloned.1.call-update) | async-done | bytes 10240016 | tf_op jit(solution)/shard_map/all_gather | solution.py:12
  240.2 34.8 %while.15 = (s32[]{:T(128)}, f32[4,200,200]{2,1,0:T(8,128)S(1)}, s32[]{:T(128)}, f32[16,4,200,200]{3,2,1,0:T(8,128)}, s32[]{:T(128)}, /*index=5*/s32[]{:T(128)}, s32[]{:T(128)}, s32[]{:T(128)}) while((s32[]{:T(128)}, f32[4,200,200]{2,1,0:T(8,128)S(1)}, s32[]{:T(128)}, f32[16,4,200,200]{3,2,1,0:T(8,128)}, s32[]{:T(128)}, /*index=5*/s32[]{:T(128)}, ...), condition=%wide.region_2.3_spmd, body=%wide.region_1.2_spmd.sunk | while | flops 384160000 | bytes 4377745 | solution.py:21
  240.3 2.1 convolution_select_fusion.2
  242.5 2.1 convolution_select_fusion.2
  244.7 2.1 convolution_select_fusion.2
  246.8 2.1 convolution_select_fusion.2
  249.0 2.1 convolution_select_fusion.2
  251.2 2.1 convolution_select_fusion.2
  253.3 2.1 convolution_select_fusion.2
  255.5 2.1 convolution_select_fusion.2
  257.7 2.1 convolution_select_fusion.2
  259.9 2.1 convolution_select_fusion.2
  262.0 2.1 convolution_select_fusion.2
  264.2 2.1 convolution_select_fusion.2
  266.4 2.1 convolution_select_fusion.2
  268.6 2.1 convolution_select_fusion.2
  280.0 36.7 %custom-call.11 = f32[4,100,100]{2,1,0:T(8,128)S(1)} custom-call(f32[4,100,100]{2,1,0:T(8,128)S(1)} %fusion.16), custom_call_target="Cholesky" | custom-call | tf_op jit(solution)/shard_map/jit(cholesky)/cholesky | solution.py:44
  317.0 31.0 %custom-call.12 = f32[4,1,100,100]{2,3,1,0:T(8,128)S(1)} custom-call(f32[4,1,100,100]{3,2,1,0:T(8,128)S(1)} %select_bitcast_fusion), custom_call_target="InvertDiagBlocksLowerTriangular" | custom-call | tf_op jit(solution)/shard_map/vmap(jit(_cho_solve))/triangular_solve | solution.py:37
  351.3 90.3 %all-reduce.4.cloned.1.call-done = f32[4,200,200]{2,1,0:T(8,128)} async-done(((f32[4,200,200]{2,1,0:T(8,128)}), f32[4,200,200]{2,1,0:T(8,128)}) %all-reduce.4.cloned.1.call-update) | async-done | bytes 640016 | tf_op jit(solution)/shard_map/psum | solution.py:84
  441.7 2.1 broadcast_multiply_fusion
  (58 shorter events, 22.5 us)
Async XLA Ops:
  6.5 57.5 %copy-start = (bf16[1,8,400]{2,1,0:T(8,128)(2,1)S(1)}, bf16[1,8,400]{2,1,0:T(8,128)(2,1)}, u32[]{:S(2)}) copy-start(bf16[1,8,400]{2,1,0:T(8,128)(2,1)} %param.6) | copy-start | bytes 19204
  6.5 119.0 %all-reduce.6.cloned.1.call-start = ((), (), s32[]{:S(2)}) async-start(), calls=%async_computation.2 | async-start | bytes 2564096
  64.0 13.5 %copy-start.3 = (u32[32]{0:T(128)S(1)}, u32[32]{0:T(128)}, u32[]{:S(2)}) copy-start(u32[32]{0:T(128)} %constant.123) | copy-start | bytes 388
  77.4 162.7 %all-gather.3.cloned.1.call-start = ((), (), s32[]{:S(2)}) async-start(), calls=%async_computation.1 | async-start | bytes 13926400 | tf_op jit(solution)/shard_map/all_gather | solution.py:12
  133.4 141.6 %copy-start.1 = (f32[200,100]{1,0:T(8,128)S(1)}, f32[200,100]{1,0:T(8,128)}, u32[]{:S(2)}) copy-start(f32[200,100]{1,0:T(8,128)} %param.8) | copy-start | bytes 240004
  136.1 141.5 %copy-start.2 = (bf16[1,4,200,100]{3,2,1,0:T(8,128)(2,1)S(1)}, bf16[1,4,200,100]{3,2,1,0:T(8,128)(2,1)}, u32[]{:S(2)}) copy-start(bf16[1,4,200,100]{3,2,1,0:T(8,128)(2,1)} %param.9) | copy-start | bytes 480004
  136.1 305.6 %all-reduce.4.cloned.1.call-start = ((), (), s32[]{:S(2)}) async-start(), calls=%async_computation | async-start | bytes 1638400 | tf_op jit(solution)/shard_map/psum | solution.py:84
Sparse Core Ops, SparseCore 0:
  77.6 47.9 all-reduce.5
  136.2 103.9 all-gather.2
  351.5 90.1 all-reduce.3
where the time goes:
time: 453 us; the launch traced here: 450 us
  waiting for transfers between devices  241 us (53%)
  other arithmetic  70.1 us (15%)
  matrix products  63.1 us (14%)
  local copies, waits for them, and re-layouts  61.3 us (14%)
  between operations  14 us (3%)
    all_gather x1, waiting for transfers between devices, entering(): everything = lax.all_gather(shard, axis)  104 us
    psum x1, waiting for transfers between devices, body(): summed = lax.psum(running, 'section')  90.3 us
    reshape x1, local copies, waits for them, and re-layouts, body(): vector_table = cholesky_vectors.reshape(chol_here, orbitals * orbitals)  57.5 us
    unnamed x4, waiting for transfers between devices  46.8 us
    another operation x4, other arithmetic, green_block(): factor = jnp.linalg.cholesky(normal_matrix)  36.9 us
    dot_general x16, matrix products, compose(): return jnp.einsum('wij,wjk->wik', later, earlier, precision=exact_mode)  33.2 us
    another operation x3, other arithmetic, solve_normal(): return jax.scipy.linalg.cho_solve((factor, True), right_side)  31.1 us
    dot_general x1, matrix products, body(): jnp.dot(field_rows, vector_table, preferred_element_type=jnp.float32)  13.4 us
  transfers between devices with their start and end apart: 3, of which 3 were waited for; matrix products, arithmetic and copies ran while one was open for 0% of the time, Pallas kernels for 0%

commit v1 on v0

--- a/solution.py
+++ b/solution.py
@@ -1,10 +1,24 @@
+import functools
 import jax
 import jax.numpy as jnp
 from jax import lax
 from jax.sharding import PartitionSpec as P
+from jax.lax import axis_size, ppermute
 
 TAYLOR = 6
 exact_mode = lax.Precision.HIGHEST
+
+
+def list_layers_all(page, along_axis):
+    nd = axis_size(along_axis)
+    arr_out = page
+    state_now = lambda formed: [(jj, jj ^ formed) for jj in range(nd)]
+    for nth in range(nd.bit_length() - 1):
+        arr_out = arr_out + ppermute(arr_out, along_axis, state_now(1 << nth))
+    return arr_out
+
+
+_wrap_sectors = functools.partial(list_layers_all, along_axis="section")
 
 
 def entering(shard, axis, combine, identity):
@@ -81,7 +95,7 @@
         left_state = jnp.einsum("wji,wje->wie", series[offset], left_state, precision=exact_mode)
         running = running + green_block(left_state, walkers[offset])
     running, leaving = (running, left_state)
-    summed = lax.psum(running, "section")
+    summed = _wrap_sectors(running)
     return summed / total_steps
 
 

time: 453 us -> 441 us (0.974)
  waiting for transfers between devices: 241 us -> 227 us
    psum x1 -> x0, waiting for transfers between devices: 90.3 us -> none  [body(): summed = lax.psum(running, 'section')]
    ppermute x0 -> x4, waiting for transfers between devices: none -> 76.6 us  [list_layers_all(): arr_out = arr_out + ppermute(arr_out, along_axis, state_now(1 << nth))]
    unnamed x4 -> x3, waiting for transfers between devices: 46.8 us -> 46.8 us
  transfers between devices with their start and end apart: 3 -> 6, of which waited for: 3 -> 6; matrix products, arithmetic and copies ran while one was open for 0% -> 0% of each run, Pallas kernels for 0% -> 0%
where the time goes in v1:
time: 441 us; the launch traced here: 438 us
  waiting for transfers between devices  227 us (51%)
  other arithmetic  69.3 us (16%)
  matrix products  62.2 us (14%)
  local copies, waits for them, and re-layouts  61.3 us (14%)
  between operations  14.3 us (3%)
    all_gather x1, waiting for transfers between devices, entering(): everything = lax.all_gather(shard, axis)  104 us
    ppermute x4, waiting for transfers between devices, list_layers_all(): arr_out = arr_out + ppermute(arr_out, along_axis, state_now(1 << nth))  76.6 us
    reshape x1, local copies, waits for them, and re-layouts, body(): vector_table = cholesky_vectors.reshape(chol_here, orbitals * orbitals)  57.5 us
    unnamed x3, waiting for transfers between devices  46.8 us
    another operation x4, other arithmetic, green_block(): factor = jnp.linalg.cholesky(normal_matrix)  36.9 us
    dot_general x16, matrix products, compose(): return jnp.einsum('wij,wjk->wik', later, earlier, precision=exact_mode)  33.2 us
    another operation x3, other arithmetic, solve_normal(): return jax.scipy.linalg.cho_solve((factor, True), right_side)  31.1 us
    dot_general x1, matrix products, body(): jnp.dot(field_rows, vector_table, preferred_element_type=jnp.float32)  13.4 us
  transfers between devices with their start and end apart: 6, of which 6 were waited for; matrix products, arithmetic and copies ran while one was open for 0% of the time, Pallas kernels for 0%

profile of v1, /device:TPU:0, one launch (start us, length us, event | category | flops | bytes accessed | tf_op | source)
XLA Modules:
  0.0 438.3 jit_solution(12323695519759260663)
XLA Ops:
  6.5 57.5 %reshape.20 = bf16[400,40000]{1,0:T(8,128)(2,1)} reshape(bf16[400,200,200]{2,1,0:T(8,128)(2,1)} %param.7) | data formatting | bytes 64000000 | tf_op jit(solution)/shard_map/reshape | solution.py:68
  64.0 13.4 %fusion.22 = f32[8,40000]{1,0:T(8,128)} fusion(bf16[400,40000]{1,0:T(8,128)(2,1)} %reshape.20, bf16[1,8,400]{2,1,0:T(8,128)(2,1)S(1)} %copy-done), kind=kOutput, calls=%fused_computation.36 | convolution fusion | flops 256000000 | bytes 33286400 | tf_op jit(solution)/shard_map/dot_general | solution.py:70
  78.8 46.8 %all-reduce.3.cloned.1.call-done = f32[8,40000]{1,0:T(8,128)} async-done(((f32[8,40000]{1,0:T(8,128)}), f32[8,40000]{1,0:T(8,128)}) %all-reduce.3.cloned.1.call-update) | async-done | bytes 1280016
  133.5 2.6 fusion.8
  136.1 104.0 %all-gather.3.cloned.1.call-done = f32[64,200,200]{2,1,0:T(8,128)} async-done(((f32[4,200,200]{2,1,0:T(8,128)}), f32[64,200,200]{2,1,0:T(8,128)}) %all-gather.3.cloned.1.call-update) | async-done | bytes 10240016 | tf_op jit(solution)/shard_map/all_gather | solution.py:26
  240.2 35.0 %while.15 = (s32[]{:T(128)}, f32[4,200,200]{2,1,0:T(8,128)S(1)}, s32[]{:T(128)}, f32[16,4,200,200]{3,2,1,0:T(8,128)}, s32[]{:T(128)}, /*index=5*/s32[]{:T(128)}, s32[]{:T(128)}, s32[]{:T(128)}) while((s32[]{:T(128)}, f32[4,200,200]{2,1,0:T(8,128)S(1)}, s32[]{:T(128)}, f32[16,4,200,200]{3,2,1,0:T(8,128)}, s32[]{:T(128)}, /*index=5*/s32[]{:T(128)}, ...), condition=%wide.region_2.3_spmd, body=%wide.region_1.2_spmd.sunk | while | flops 384160000 | bytes 4377745 | solution.py:35
  242.7 2.1 convolution_select_fusion.2
  244.8 2.1 convolution_select_fusion.2
  247.0 2.1 convolution_select_fusion.2
  249.2 2.1 convolution_select_fusion.2
  251.4 2.1 convolution_select_fusion.2
  253.5 2.1 convolution_select_fusion.2
  257.9 2.1 convolution_select_fusion.2
  260.1 2.1 convolution_select_fusion.2
  262.2 2.1 convolution_select_fusion.2
  264.4 2.1 convolution_select_fusion.2
  266.6 2.1 convolution_select_fusion.2
  268.8 2.1 convolution_select_fusion.2
  270.9 2.1 convolution_select_fusion.2
  280.2 36.7 %custom-call.11 = f32[4,100,100]{2,1,0:T(8,128)S(1)} custom-call(f32[4,100,100]{2,1,0:T(8,128)S(1)} %fusion.16), custom_call_target="Cholesky" | custom-call | tf_op jit(solution)/shard_map/jit(cholesky)/cholesky | solution.py:58
  317.2 31.0 %custom-call.12 = f32[4,1,100,100]{2,3,1,0:T(8,128)S(1)} custom-call(f32[4,1,100,100]{3,2,1,0:T(8,128)S(1)} %select_bitcast_fusion), custom_call_target="InvertDiagBlocksLowerTriangular" | custom-call | tf_op jit(solution)/shard_map/vmap(jit(_cho_solve))/triangular_solve | solution.py:51
  353.8 19.8 %collective-permute-done.1 = f32[4,200,200]{2,1,0:T(8,128)S(1)} collective-permute-done((f32[4,200,200]{2,1,0:T(8,128)S(1)}, f32[4,200,200]{2,1,0:T(8,128)S(1)}, u32[]{:S(2)}, u32[]{:S(2)}) %collective-permute-start.1) | collective-permute-done | bytes 640032 | tf_op jit(solution)/shard_map/ppermute | solution.py:17
  374.1 19.2 %collective-permute-done.2 = f32[4,200,200]{2,1,0:T(8,128)S(1)} collective-permute-done((f32[4,200,200]{2,1,0:T(8,128)S(1)}, f32[4,200,200]{2,1,0:T(8,128)S(1)}, u32[]{:S(2)}, u32[]{:S(2)}) %collective-permute-start.2) | collective-permute-done | bytes 640032 | tf_op jit(solution)/shard_map/ppermute | solution.py:17
  395.0 35.4 %collective-permute-done.3 = f32[4,200,200]{2,1,0:T(8,128)S(1)} collective-permute-done((f32[4,200,200]{2,1,0:T(8,128)S(1)}, f32[4,200,200]{2,1,0:T(8,128)S(1)}, u32[]{:S(2)}, u32[]{:S(2)}) %collective-permute-start.3) | collective-permute-done | bytes 640032 | tf_op jit(solution)/shard_map/ppermute | solution.py:17
  (68 shorter events, 29.7 us)
Async XLA Ops:
  6.5 57.5 %copy-start = (bf16[1,8,400]{2,1,0:T(8,128)(2,1)S(1)}, bf16[1,8,400]{2,1,0:T(8,128)(2,1)}, u32[]{:S(2)}) copy-start(bf16[1,8,400]{2,1,0:T(8,128)(2,1)} %param.6) | copy-start | bytes 19204
  6.5 119.0 %all-reduce.3.cloned.1.call-start = ((), (), s32[]{:S(2)}) async-start(), calls=%async_computation.1 | async-start | bytes 2564096
  64.0 13.5 %copy-start.4 = (u32[32]{0:T(128)S(1)}, u32[32]{0:T(128)}, u32[]{:S(2)}) copy-start(u32[32]{0:T(128)} %constant.123) | copy-start | bytes 388
  77.4 162.7 %all-gather.3.cloned.1.call-start = ((), (), s32[]{:S(2)}) async-start(), calls=%async_computation | async-start | bytes 13926400 | tf_op jit(solution)/shard_map/all_gather | solution.py:26
  133.5 141.8 %copy-start.2 = (f32[200,100]{1,0:T(8,128)S(1)}, f32[200,100]{1,0:T(8,128)}, u32[]{:S(2)}) copy-start(f32[200,100]{1,0:T(8,128)} %param.8) | copy-start | bytes 240004
  136.1 141.7 %copy-start.3 = (bf16[1,4,200,100]{3,2,1,0:T(8,128)(2,1)S(1)}, bf16[1,4,200,100]{3,2,1,0:T(8,128)(2,1)}, u32[]{:S(2)}) copy-start(bf16[1,4,200,100]{3,2,1,0:T(8,128)(2,1)} %param.9) | copy-start | bytes 480004
  275.2 156.2 %copy-start.1 = (bf16[1,8,400]{2,1,0:T(8,128)(2,1)S(1)}, bf16[1,8,400]{2,1,0:T(8,128)(2,1)}, u32[]{:S(2)}) copy-start(bf16[1,8,400]{2,1,0:T(8,128)(2,1)} %param.6) | copy-start | bytes 19204
  350.6 2.4 collective-permute-start
  353.2 20.5 %collective-permute-start.1 = (f32[4,200,200]{2,1,0:T(8,128)S(1)}, f32[4,200,200]{2,1,0:T(8,128)S(1)}, u32[]{:S(2)}, u32[]{:S(2)}) collective-permute-start(f32[4,200,200]{2,1,0:T(8,128)S(1)} %add.94), channel_id=1, source_target_pairs={{0,4},{2,6},{4,0},{6,2},{8,12},{10,14},{12,8},{14,10},{16,20},{18,... | collective-permute-start | bytes 1920008 | tf_op jit(solution)/shard_map/ppermute | solution.py:17
  373.7 19.6 %collective-permute-start.2 = (f32[4,200,200]{2,1,0:T(8,128)S(1)}, f32[4,200,200]{2,1,0:T(8,128)S(1)}, u32[]{:S(2)}, u32[]{:S(2)}) collective-permute-start(f32[4,200,200]{2,1,0:T(8,128)S(1)} %add.95), channel_id=1, source_target_pairs={{0,8},{2,10},{4,12},{6,14},{8,0},{10,2},{12,4},{14,6},{16,24},{18,... | collective-permute-start | bytes 1920008 | tf_op jit(solution)/shard_map/ppermute | solution.py:17
  393.5 37.0 %collective-permute-start.3 = (f32[4,200,200]{2,1,0:T(8,128)S(1)}, f32[4,200,200]{2,1,0:T(8,128)S(1)}, u32[]{:S(2)}, u32[]{:S(2)}) collective-permute-start(f32[4,200,200]{2,1,0:T(8,128)S(1)} %add.96), channel_id=1, source_target_pairs={{0,16},{2,18},{4,20},{6,22},{8,24},{10,26},{12,28},{14,30},{16,0},... | collective-permute-start | bytes 1920008 | tf_op jit(solution)/shard_map/ppermute | solution.py:17
Sparse Core Ops, SparseCore 0:
  77.6 47.9 all-reduce.2
  136.2 103.9 all-gather.2
